TPU v7x, 128 devices: a whole 4x4x4 slice. The times are simulated.
128 devices in a mesh: dp: 1, sp: 128 (over z, y, x, core).
Axes of the slice: x: 4, y: 4, z: 4, core: 2. Of those that a mesh axis runs over, the one named last changes fastest.
Arguments:
- y_dec: bfloat16 [2048, 768], P(('dp', 'sp'))
- memory: bfloat16 [131072, 768], P(('dp', 'sp'))
- mem_len: int32 [1], P('dp')
- norm_gain: bfloat16 [2, 768], replicated
- self_wq: bfloat16 [2, 768, 768], replicated
- self_wk: bfloat16 [2, 768, 768], replicated
- self_wv: bfloat16 [2, 768, 768], replicated
- self_wo: bfloat16 [2, 768, 768], replicated
- cross_wq: bfloat16 [2, 768, 768], replicated
- cross_wk: bfloat16 [2, 768, 768], replicated
- cross_wv: bfloat16 [2, 768, 768], replicated
- cross_wo: bfloat16 [2, 768, 768], replicated
- mlp_gate: bfloat16 [2, 768, 2048], replicated
- mlp_up: bfloat16 [2, 768, 2048], replicated
- mlp_down: bfloat16 [2, 2048, 768], replicated
Outputs:
- output: bfloat16 [2048, 768], P(('dp', 'sp'))
All inputs are finite; a program needn't handle non-finite values.
Results may differ from a plain program's by a relative error of at most 0.0105201.
Values are sent between devices in bfloat16 or wider.
A program may use at most 1 GiB of HBM per device.

v0:
```python
import jax
import jax.numpy as jnp
from jax import lax
from jax.sharding import PartitionSpec as P

HEAD = 64
NORM_EPS = 1e-6
NEG_BIG = -1e30


def matmul(left_mat, right_mat):
    return jnp.dot(left_mat, right_mat, preferred_element_type=jnp.float32)


def rms_norm(hidden, gain_vec):
    wide_vals = hidden.astype(jnp.float32)
    inv_rms = lax.rsqrt(jnp.mean(wide_vals * wide_vals, axis=-1, keepdims=True) + NORM_EPS)
    return (wide_vals * inv_rms * gain_vec.astype(jnp.float32)).astype(jnp.bfloat16)


def solution(mesh):
    group_size = mesh.shape["sp"]
    row_spec = P(("dp", "sp"), None)
    full_spec = P()

    def device_step(y_dec, memory, mem_len, norm_gain, self_wq, self_wk, self_wv, self_wo, cross_wq, cross_wk, cross_wv, cross_wo, mlp_gate, mlp_up, mlp_down):
        tq_dev, width = y_dec.shape
        tm_dev = memory.shape[0]
        num_heads = width // HEAD
        kv_heads = cross_wk.shape[2] // HEAD
        q_group = num_heads // kv_heads
        tq_all = tq_dev * group_size
        score_scale = HEAD ** -0.5
        shard_idx = lax.axis_index("sp")
        query_pos = shard_idx * tq_dev + jnp.arange(tq_dev)
        causal = jnp.arange(tq_all)[None, :] <= query_pos[:, None]
        mem_valid = shard_idx * tm_dev + jnp.arange(tm_dev) < mem_len[0]
        hidden = y_dec
        for layer_idx in range(norm_gain.shape[0]):
            normed = rms_norm(hidden, norm_gain[layer_idx])
            query_self = matmul(normed, self_wq[layer_idx]).astype(jnp.bfloat16).reshape(tq_dev, num_heads, HEAD)
            key_local = matmul(normed, self_wk[layer_idx]).astype(jnp.bfloat16)
            value_local = matmul(normed, self_wv[layer_idx]).astype(jnp.bfloat16)
            key_self = lax.all_gather(key_local, "sp", axis=0, tiled=True).reshape(tq_all, num_heads, HEAD)
            value_self = lax.all_gather(value_local, "sp", axis=0, tiled=True).reshape(tq_all, num_heads, HEAD)
            scores = jnp.einsum("qhd,khd->hqk", query_self, key_self, preferred_element_type=jnp.float32) * score_scale
            scores = jnp.where(causal, scores, NEG_BIG)
            self_probs = jax.nn.softmax(scores, axis=-1).astype(jnp.bfloat16)
            self_heads = jnp.einsum("hqk,khd->qhd", self_probs, value_self, preferred_element_type=jnp.float32)
            self_part = matmul(self_heads.astype(jnp.bfloat16).reshape(tq_dev, width), self_wo[layer_idx])

            query_local = matmul(normed, cross_wq[layer_idx]).astype(jnp.bfloat16)
            query_cross = lax.all_gather(query_local, "sp", axis=0, tiled=True).reshape(tq_all, kv_heads, q_group, HEAD)
            key_mem = matmul(memory, cross_wk[layer_idx]).astype(jnp.bfloat16).reshape(tm_dev, kv_heads, HEAD)
            value_mem = matmul(memory, cross_wv[layer_idx]).astype(jnp.bfloat16).reshape(tm_dev, kv_heads, HEAD)
            scores = jnp.einsum("qkgd,mkd->kgqm", query_cross, key_mem, preferred_element_type=jnp.float32) * score_scale
            scores = jnp.where(mem_valid, scores, NEG_BIG)
            part_max = jnp.max(scores, axis=-1)
            weights = jnp.exp(scores - part_max[..., None])
            part_sum = jnp.sum(weights, axis=-1)
            part_out = jnp.einsum("kgqm,mkd->kgqd", weights.astype(jnp.bfloat16), value_mem, preferred_element_type=jnp.float32)
            top_max = lax.pmax(part_max, "sp")
            rescale = jnp.exp(part_max - top_max)
            numerator = lax.psum_scatter(part_out * rescale[..., None], "sp", scatter_dimension=2, tiled=True)
            denominator = lax.psum_scatter(part_sum * rescale, "sp", scatter_dimension=2, tiled=True)
            cross_heads = (numerator / denominator[..., None]).astype(jnp.bfloat16)
            cross_flat = jnp.transpose(cross_heads, (2, 0, 1, 3)).reshape(tq_dev, width)
            cross_part = matmul(cross_flat, cross_wo[layer_idx])

            activated = (jax.nn.silu(matmul(normed, mlp_gate[layer_idx])) * matmul(normed, mlp_up[layer_idx])).astype(jnp.bfloat16)
            mlp_part = matmul(activated, mlp_down[layer_idx])
            hidden = (hidden.astype(jnp.float32) + self_part + cross_part + mlp_part).astype(jnp.bfloat16)
        return hidden

    return jax.shard_map(device_step, mesh=mesh, in_specs=(row_spec, row_spec, P("dp")) + (full_spec,) * 12, out_specs=row_spec, check_vma=False)
```

profile of v0, /device:TPU:1, one launch (start us, length us, event | category | flops | bytes accessed | tf_op | source)
XLA Modules:
  0.0 2425.8 jit_solution(9230946644916881875)
XLA Ops:
  13.9 66.1 %all-gather.11.cloned.1.call-done = bf16[2048,768]{1,0:T(8,128)(2,1)} async-done(((bf16[16,768]{1,0:T(8,128)(2,1)}), bf16[2048,768]{1,0:T(8,128)(2,1)}) %all-gather.11.cloned.1.call-update) | async-done | bytes 3145744 | tf_op jit(solution)/shard_map/all_gather | solution.py:53
  80.0 4.7 copy.58
  84.7 37.6 %bitcast_reduce_fusion.1 = (f32[12,2048]{1,0:T(8,128)}, f32[12,1024,2048]{2,1,0:T(8,128)}) fusion(pred[1024]{0:T(1024)(128)(4,1)S(1)} %add_compare_fusion, bf16[1024,12,64]{0,2,1:T(8,128)(2,1)S(1)} %bitcast.278, bf16[2048,12,64]{0,2,1:T(8,128)(2,1)} %bitcast.268), kind=kOutput, calls=%fused_computation.7 | convolution fusion | flops 3296698368 | bytes 105481216 | tf_op jit(solution)/shard_map/qkgd,mkd->kgqm/dot_general | solution.py:56
  127.0 3.9 convolution_convert_fusion.2
  130.9 31.3 %fusion.4 = f32[12,2048]{1,0:T(8,128)S(1)} fusion(f32[12,1024,2048]{2,1,0:T(8,128)} %get-tuple-element.12, f32[12,2048]{1,0:T(8,128)S(1)} %copy-done.2, pred[1024]{0:T(1024)(128)(4,1)S(1)} %add_compare_fusion), kind=kLoop, calls=%fused_computation.10 | loop fusion | flops 100638720 | bytes 100860928 | tf_op jit(solution)/shard_map/reduce_sum | solution.py:60
  162.1 103.7 %all-reduce.7.cloned.1.call-done = f32[12,1,2048]{2,0,1:T(8,128)} async-done(((f32[12,1,2048]{2,0,1:T(8,128)}), f32[12,1,2048]{2,0,1:T(8,128)}) %all-reduce.7.cloned.1.call-update) | async-done | bytes 98320 | tf_op jit(solution)/shard_map/pmax | solution.py:62
  268.9 36.5 %multiply_bitcast_fusion.1 = f32[12,1,2048,64]{2,3,0,1:T(8,128)} fusion(bf16[1024,12,64]{0,2,1:T(8,128)(2,1)} %bitcast.283, f32[12,1024,2048]{2,1,0:T(8,128)} %get-tuple-element.12, f32[12,2048]{1,0:T(8,128)S(1)} %copy-done.2, pred[1024]{0:T(1024)(128)(4,1)S(1)} %add_compare_fusion, f32[12,2048]{1,0:T(8,128)S(1)} %get-tuple-element.10), kind=kOutput, calls=%fused_computation.21 | convolution fusion | flops 3323461632 | bytes 108725248 | tf_op jit(solution)/shard_map/kgqm,mkd->kgqd/dot_general | solution.py:61
  305.4 29.8 %copy.60 = f32[12,1,2048,64]{3,1,0,2:T(1,128)} copy(f32[12,1,2048,64]{2,3,0,1:T(8,128)} %multiply_bitcast_fusion.1) | data formatting | bytes 12582912 | tf_op jit(solution)/shard_map/mul | solution.py:64
  339.5 3.9 fusion.26
  343.5 4.7 copy.55
  348.2 51.4 %all-gather.7.cloned.1.call-done = bf16[2048,768]{1,0:T(8,128)(2,1)} async-done(((bf16[16,768]{1,0:T(8,128)(2,1)}), bf16[2048,768]{1,0:T(8,128)(2,1)}) %all-gather.7.cloned.1.call-update) | async-done | bytes 3145744 | tf_op jit(solution)/shard_map/all_gather | solution.py:45
  399.5 4.7 copy.54
  404.2 2.7 fusion.191
  407.0 2.9 fusion.100
  410.0 628.1 %reduce-scatter.7.cloned.1.call-done = f32[16,12]{1,0:T(8,128)} async-done(((f32[2048,12]{1,0:T(8,128)}), f32[16,12]{1,0:T(8,128)}) %reduce-scatter.7.cloned.1.call-update) | async-done | bytes 784
  1038.1 173.0 %all-reduce.11.cloned.1.call-done = f32[12,1,2048,64]{3,1,0,2:T(1,128)} async-done(((f32[12,1,2048,64]{3,1,0,2:T(1,128)}), f32[12,1,2048,64]{3,1,0,2:T(1,128)}) %all-reduce.11.cloned.1.call-update) | async-done | bytes 6291472
  1218.3 2.7 convolution_convert_fusion.1
  1221.0 61.6 %all-gather.17.cloned.1.call-done = bf16[2048,768]{1,0:T(8,128)(2,1)} async-done(((bf16[16,768]{1,0:T(8,128)(2,1)}), bf16[2048,768]{1,0:T(8,128)(2,1)}) %all-gather.17.cloned.1.call-update) | async-done | bytes 3145744 | tf_op jit(solution)/shard_map/all_gather | solution.py:53
  1282.6 4.7 copy.66
  1287.3 37.6 %bitcast_reduce_fusion = (f32[12,2048]{1,0:T(8,128)}, f32[12,1024,2048]{2,1,0:T(8,128)}) fusion(pred[1024]{0:T(1024)(128)(4,1)S(1)} %add_compare_fusion, bf16[1024,12,64]{0,2,1:T(8,128)(2,1)S(1)} %bitcast.279, bf16[2048,12,64]{0,2,1:T(8,128)(2,1)} %bitcast.269), kind=kOutput, calls=%fused_computation.3 | convolution fusion | flops 3296698368 | bytes 105481216 | tf_op jit(solution)/shard_map/qkgd,mkd->kgqm/dot_general | solution.py:56
  1327.2 4.0 convolution_convert_fusion
  1332.2 31.3 %fusion.6 = f32[12,2048]{1,0:T(8,128)S(1)} fusion(f32[12,1024,2048]{2,1,0:T(8,128)} %get-tuple-element.18, f32[12,2048]{1,0:T(8,128)S(1)} %copy-done.1, pred[1024]{0:T(1024)(128)(4,1)S(1)} %add_compare_fusion), kind=kLoop, calls=%fused_computation.12 | loop fusion | flops 100638720 | bytes 100860928 | tf_op jit(solution)/shard_map/reduce_sum | solution.py:60
  1363.5 104.9 %all-reduce.9.cloned.1.call-done = f32[12,1,2048]{2,0,1:T(8,128)} async-done(((f32[12,1,2048]{2,0,1:T(8,128)}), f32[12,1,2048]{2,0,1:T(8,128)}) %all-reduce.9.cloned.1.call-update) | async-done | bytes 98320 | tf_op jit(solution)/shard_map/pmax | solution.py:62
  1471.5 36.5 %multiply_bitcast_fusion = f32[12,1,2048,64]{2,3,0,1:T(8,128)} fusion(bf16[1024,12,64]{0,2,1:T(8,128)(2,1)} %bitcast.282, f32[12,1024,2048]{2,1,0:T(8,128)} %get-tuple-element.18, f32[12,2048]{1,0:T(8,128)S(1)} %copy-done.1, pred[1024]{0:T(1024)(128)(4,1)S(1)} %add_compare_fusion, f32[12,2048]{1,0:T(8,128)S(1)} %get-tuple-element.8), kind=kOutput, calls=%fused_computation.20 | convolution fusion | flops 3323461632 | bytes 108725248 | tf_op jit(solution)/shard_map/kgqm,mkd->kgqd/dot_general | solution.py:61
  1508.0 29.8 %copy.68 = f32[12,1,2048,64]{3,1,0,2:T(1,128)} copy(f32[12,1,2048,64]{2,3,0,1:T(8,128)} %multiply_bitcast_fusion) | data formatting | bytes 12582912 | tf_op jit(solution)/shard_map/mul | solution.py:64
  1541.9 3.9 fusion.20
  1545.8 4.7 copy.63
  1550.5 51.7 %all-gather.13.cloned.1.call-done = bf16[2048,768]{1,0:T(8,128)(2,1)} async-done(((bf16[16,768]{1,0:T(8,128)(2,1)}), bf16[2048,768]{1,0:T(8,128)(2,1)}) %all-gather.13.cloned.1.call-update) | async-done | bytes 3145744 | tf_op jit(solution)/shard_map/all_gather | solution.py:45
  1602.2 4.7 copy.62
  1609.6 2.9 fusion.101
  1612.6 628.3 %reduce-scatter.9.cloned.1.call-done = f32[16,12]{1,0:T(8,128)} async-done(((f32[2048,12]{1,0:T(8,128)}), f32[16,12]{1,0:T(8,128)}) %reduce-scatter.9.cloned.1.call-update) | async-done | bytes 784
  2240.9 172.9 %all-reduce.13.cloned.1.call-done = f32[12,1,2048,64]{3,1,0,2:T(1,128)} async-done(((f32[12,1,2048,64]{3,1,0,2:T(1,128)}), f32[12,1,2048,64]{3,1,0,2:T(1,128)}) %all-reduce.13.cloned.1.call-update) | async-done | bytes 6291472
  (74 shorter events, 44.4 us)
Async XLA Ops:
  6.5 4.7 copy-start
  6.5 73.5 %all-gather.11.cloned.1.call-start = ((), (), s32[]{:S(2)}) async-start(), calls=%async_computation.4 | async-start | bytes 3170304 | tf_op jit(solution)/shard_map/all_gather | solution.py:53
  10.5 255.3 %all-reduce.7.cloned.1.call-start = ((), (), s32[]{:S(2)}) async-start(), calls=%async_computation.5 | async-start | bytes 262144 | tf_op jit(solution)/shard_map/pmax | solution.py:62
  84.7 37.7 %copy-start.4 = (bf16[16,768]{1,0:T(8,128)(2,1)S(1)}, bf16[16,768]{1,0:T(8,128)(2,1)}, u32[]{:S(2)}) copy-start(bf16[16,768]{1,0:T(8,128)(2,1)} %param.15) | copy-start | bytes 73732
  122.3 221.1 %all-gather.9.cloned.1.call-start = ((), (), s32[]{:S(2)}) async-start(), calls=%async_computation.3 | async-start | bytes 3170304 | tf_op jit(solution)/shard_map/all_gather | solution.py:44
  124.6 274.9 %all-gather.7.cloned.1.call-start = ((), (), s32[]{:S(2)}) async-start(), calls=%async_computation.2 | async-start | bytes 3170304 | tf_op jit(solution)/shard_map/all_gather | solution.py:45
  126.9 4.0 copy-start.2
  126.9 911.2 %reduce-scatter.7.cloned.1.call-start = ((), (), s32[]{:S(2)}) async-start(), calls=%async_computation.10 | async-start | bytes 1056768
  268.6 942.5 %all-reduce.11.cloned.1.call-start = ((), (), s32[]{:S(2)}) async-start(), calls=%async_computation.12 | async-start | bytes 25165824
  335.2 947.4 %all-gather.17.cloned.1.call-start = ((), (), s32[]{:S(2)}) async-start(), calls=%async_computation.8 | async-start | bytes 3170304 | tf_op jit(solution)/shard_map/all_gather | solution.py:53
  1218.0 250.3 %all-reduce.9.cloned.1.call-start = ((), (), s32[]{:S(2)}) async-start(), calls=%async_computation.9 | async-start | bytes 262144 | tf_op jit(solution)/shard_map/pmax | solution.py:62
  1324.9 221.0 %all-gather.15.cloned.1.call-start = ((), (), s32[]{:S(2)}) async-start(), calls=%async_computation.7 | async-start | bytes 3170304 | tf_op jit(solution)/shard_map/all_gather | solution.py:44
  1327.1 5.1 copy-start.1
  1327.1 275.1 %all-gather.13.cloned.1.call-start = ((), (), s32[]{:S(2)}) async-start(), calls=%async_computation.6 | async-start | bytes 3170304 | tf_op jit(solution)/shard_map/all_gather | solution.py:45
  1327.2 4.0 copy-start.3
  1332.1 908.8 %reduce-scatter.9.cloned.1.call-start = ((), (), s32[]{:S(2)}) async-start(), calls=%async_computation.11 | async-start | bytes 1056768
  1471.2 942.6 %all-reduce.13.cloned.1.call-start = ((), (), s32[]{:S(2)}) async-start(), calls=%async_computation.13 | async-start | bytes 25165824
Sparse Core Ops, SparseCore 0:
  10.6 69.3 all-gather.10
  122.5 143.2 all-reduce.6
  268.9 64.5 all-gather.8
  336.4 63.0 all-gather.6
  401.7 636.3 reduce-scatter.6
  1042.9 168.1 all-reduce.10
  1218.1 64.3 all-gather.16
  1325.0 143.3 all-reduce.8
  1471.5 64.5 all-gather.14
  1539.1 63.0 all-gather.12
  1604.5 636.3 reduce-scatter.8
  2245.7 168.1 all-reduce.12
where the time goes:
time: 2430 us
  waiting for transfers between devices  2040 us (84%)
  matrix products  207 us (9%)
  local copies, waits for them, and re-layouts  92.3 us (4%)
  other arithmetic  68.8 us (3%)
    unnamed x16, waiting for transfers between devices  1600 us
    pmax x2, waiting for transfers between devices, device_step(): top_max = lax.pmax(part_max, 'sp')  209 us
    all_gather x2, waiting for transfers between devices, device_step(): lax.all_gather(query_local, 'sp', axis=0, tiled=True)  128 us
    all_gather x2, waiting for transfers between devices, device_step(): lax.all_gather(value_local, 'sp', axis=0, tiled=True)  103 us
    dot_general x2, matrix products, device_step(): jnp.einsum('qkgd,mkd->kgqm', query_cross, key_mem, preferred_element_type...  75.2 us
    dot_general x2, matrix products, device_step(): jnp.einsum('kgqm,mkd->kgqd', weights.astype(jnp.bfloat16), value_mem, pre...  73.1 us
    reduce_sum x2, other arithmetic, device_step(): part_sum = jnp.sum(weights, axis=-1)  62.5 us
    mul x2, local copies, waits for them, and re-layouts, device_step(): part_out * rescale[..., None]  59.6 us
  transfers between devices with their start and end apart: 12, of which 10 were waited for; matrix products, arithmetic and copies ran while one was open for 11% of the time, Pallas kernels for 0%

commit v1 on v0

v1 whole, which is shorter than its diff:
```python
import functools
import math

import jax
import jax.numpy as jnp
from jax import lax
from jax.experimental import pallas as pl
from jax.experimental.pallas import tpu as pltpu
from jax.sharding import PartitionSpec as P

HEAD = 64
NORM_EPS = 1e-6
NEG_BIG = -1e30
MESH = pl.DeviceIdType.MESH
EXP_SCALE = HEAD ** -0.5 * math.log2(math.e)
ORDERS = ((0, 1, 2), (1, 2, 0), (2, 0, 1))
VMEM_SPEC = pl.BlockSpec(memory_space=pltpu.VMEM)
ROW_TILE = 512


def matmul(left_mat, right_mat):
    return jnp.dot(left_mat, right_mat, preferred_element_type=jnp.float32)


def rms_norm(hidden, gain_vec):
    wide_vals = hidden.astype(jnp.float32)
    inv_rms = lax.rsqrt(jnp.mean(wide_vals * wide_vals, axis=-1, keepdims=True) + NORM_EPS)
    return (wide_vals * inv_rms * gain_vec.astype(jnp.float32)).astype(jnp.bfloat16)


def coords():
    sp = lax.axis_index("sp")
    return (sp // 32, (sp // 8) % 4, (sp // 2) % 4), sp % 2


def device_of(pos, core):
    return {"sp": ((pos[0] * 4 + pos[1]) * 4 + pos[2]) * 2 + core}


def shifted(pos, axis, dist):
    return tuple((c + dist) % 4 if i == axis else c for i, c in enumerate(pos))


def entry_barrier(pos, core):
    sem = pltpu.get_barrier_semaphore()
    for axis in range(3):
        for dist in (1, 2, 3):
            pl.semaphore_signal(sem, inc=1, device_id=device_of(shifted(pos, axis, dist), core), device_id_type=MESH)
    pl.semaphore_signal(sem, inc=1, device_id=device_of(pos, 1 - core), device_id_type=MESH)
    pl.semaphore_wait(sem, 10)


def swap_kernel(mem_ref, out_ref, local_sem, send_sem, recv_sem):
    pos, core = coords()
    sem = pltpu.get_barrier_semaphore()
    other = device_of(pos, 1 - core)
    pl.semaphore_signal(sem, inc=1, device_id=other, device_id_type=MESH)
    pl.semaphore_wait(sem, 1)
    remote = pltpu.make_async_remote_copy(
        src_ref=mem_ref, dst_ref=out_ref.at[core], send_sem=send_sem, recv_sem=recv_sem,
        device_id=other, device_id_type=MESH)
    remote.start()
    local = pltpu.make_async_copy(mem_ref, out_ref.at[core], local_sem)
    local.start()
    local.wait()
    remote.wait()


def swap_memory(memory):
    rows, width = memory.shape
    return pl.pallas_call(
        swap_kernel,
        out_shape=jax.ShapeDtypeStruct((2, rows, width), memory.dtype),
        in_specs=[VMEM_SPEC],
        out_specs=pl.BlockSpec(memory_space=pl.ANY),
        scratch_shapes=[pltpu.SemaphoreType.DMA] * 3,
        compiler_params=pltpu.CompilerParams(collective_id=0, has_side_effects=True),
        name="swap_memory",
    )(memory)


def gather_slice(ref, part, order, free, pos, core):
    idx = [part]
    for axis in range(3):
        idx.append(slice(None) if axis in free else pos[axis])
    return ref.at[tuple(idx) + (core,)]


def gather_kernel(x_ref, out_ref, local_sem, send_sem, recv_sem, sib_send, sib_recv):
    pos, core = coords()
    entry_barrier(pos, core)
    sibling = device_of(pos, 1 - core)

    def phase_copy(part, phase, dist):
        order = ORDERS[part]
        if phase == 0:
            src = x_ref.at[part]
        else:
            src = gather_slice(out_ref, part, order, order[:phase], pos, core)
        dst = gather_slice(out_ref, part, order, order[:phase], pos, core)
        return pltpu.make_async_remote_copy(
            src_ref=src, dst_ref=dst, send_sem=send_sem.at[part, phase, dist - 1],
            recv_sem=recv_sem.at[part, phase, dist - 1],
            device_id=device_of(shifted(pos, order[phase], dist), core), device_id_type=MESH)

    def sibling_copy(part, dist):
        order = ORDERS[part]
        at = shifted(pos, order[2], 4 - dist)
        ref = gather_slice(out_ref, part, order, order[:2], at, core)
        return pltpu.make_async_remote_copy(
            src_ref=ref, dst_ref=ref, send_sem=sib_send.at[part, dist], recv_sem=sib_recv.at[part, dist],
            device_id=sibling, device_id_type=MESH)

    local = [pltpu.make_async_copy(x_ref.at[p], gather_slice(out_ref, p, ORDERS[p], (), pos, core), local_sem.at[p])
             for p in range(3)]
    copies = {}
    for phase in range(3):
        for part in range(3):
            if phase == 1:
                local[part].wait()
            if phase > 0:
                for dist in (1, 2, 3):
                    copies[part, phase - 1, dist].wait_recv()
            for dist in (2, 1, 3):
                copies[part, phase, dist] = phase_copy(part, phase, dist)
                copies[part, phase, dist].start()
            if phase == 0:
                local[part].start()
            if phase == 2:
                copies[part, 3, 0] = sibling_copy(part, 0)
                copies[part, 3, 0].start()
    for dist in (1, 3, 2):
        for part in range(3):
            copies[part, 2, dist].wait_recv()
            copies[part, 3, dist] = sibling_copy(part, dist)
            copies[part, 3, dist].start()
    for part in range(3):
        for dist in range(4):
            copies[part, 3, dist].wait_recv()
    for copy in copies.values():
        copy.wait_send()


def gather_rows(normed):
    rows, width = normed.shape
    parts = normed.reshape(rows, 3, width // 3).transpose(1, 0, 2)
    gathered = pl.pallas_call(
        gather_kernel,
        out_shape=jax.ShapeDtypeStruct((3, 4, 4, 4, 2, rows, width // 3), normed.dtype),
        in_specs=[VMEM_SPEC],
        out_specs=VMEM_SPEC,
        scratch_shapes=[pltpu.SemaphoreType.DMA((3,)), pltpu.SemaphoreType.DMA((3, 3, 3)),
                        pltpu.SemaphoreType.DMA((3, 3, 3)), pltpu.SemaphoreType.DMA((3, 4)),
                        pltpu.SemaphoreType.DMA((3, 4))],
        compiler_params=pltpu.CompilerParams(collective_id=1, has_side_effects=True),
        name="gather_rows",
    )(parts)
    return gathered.reshape(3, 4, 4, 4, 2 * rows, width // 3)


def self_kernel(info_ref, h_ref, wq_ref, wk_ref, wv_ref, cq_ref, att_ref, qt_ref, k_ref, v_ref):
    core_heads = wq_ref.shape[1]
    chip = info_ref[0]
    hz, hy, hx = chip // 16, (chip // 4) % 4, chip % 4

    def rows_cat(z, y, x):
        return jnp.concatenate([h_ref[p, z, y, x] for p in range(3)], axis=1)

    def key_tile(zy, carry):
        z, y = zy // 4, zy % 4
        rows = jnp.concatenate([rows_cat(z, y, x) for x in range(4)], axis=0)
        at = pl.ds(pl.multiple_of(zy * 128, 128), 128)
        k_ref[at, :] = matmul(rows, wk_ref[...]).astype(jnp.bfloat16)
        v_ref[at, :] = matmul(rows, wv_ref[...]).astype(jnp.bfloat16)
        return carry

    lax.fori_loop(0, 16, key_tile, 0)

    for part in range(3):
        cols = slice(part * 128, part * 128 + 128)

        def query_tile(ab, carry, part=part, cols=cols):
            order = ORDERS[part]
            blocks = []
            for c in range(4):
                at = [None] * 3
                at[order[0]], at[order[1]], at[order[2]] = ab // 4, ab % 4, c
                blocks.append(rows_cat(*at))
            rows = jnp.concatenate(blocks, axis=0)
            q = matmul(rows, cq_ref[:, cols])
            qt_ref[part, ab] = jnp.transpose(q).astype(jnp.bfloat16)
            return carry

        lax.fori_loop(0, 16, query_tile, 0)

    rows = rows_cat(hz, hy, hx)
    query = matmul(rows, wq_ref[...]).astype(jnp.bfloat16)
    n_query = rows.shape[0]
    n_keys = k_ref.shape[0]
    low = lax.broadcasted_iota(jnp.int32, (n_query, 128), 1) < HEAD
    key_pos = lax.broadcasted_iota(jnp.int32, (n_query, n_keys), 1)
    query_pos = chip * n_query + lax.broadcasted_iota(jnp.int32, (n_query, n_keys), 0)
    causal = key_pos <= query_pos
    for part in range(core_heads // 128):
        cols = slice(part * 128, part * 128 + 128)
        q_pair = query[:, cols]
        outs = []
        for head in range(2):
            mask = low if head == 0 else jnp.logical_not(low)
            q_one = jnp.where(mask, q_pair, jnp.zeros_like(q_pair))
            s = lax.dot_general(q_one, k_ref[:, cols], (((1,), (1,)), ((), ())), preferred_element_type=jnp.float32)
            s = jnp.where(causal, s, NEG_BIG)
            top = jnp.max(s, axis=1, keepdims=True)
            w = jnp.exp2((s - top) * EXP_SCALE)
            total = jnp.sum(w, axis=1, keepdims=True)
            o = matmul(w.astype(jnp.bfloat16), v_ref[:, cols])
            outs.append(o / total)
        att_ref[:, cols] = jnp.where(low, outs[0], outs[1]).astype(jnp.bfloat16)


def self_attention(info, gathered, layer, wq, wk, wv, cq):
    width = wq.shape[1]
    half = width // 2
    n_rows = 64 * gathered.shape[4]
    w_spec = pl.BlockSpec((None, width, half), lambda i, info: (layer, 0, info[1]))
    return pl.pallas_call(
        self_kernel,
        grid_spec=pltpu.PrefetchScalarGridSpec(
            num_scalar_prefetch=1,
            grid=(1,),
            in_specs=[pl.BlockSpec(gathered.shape, lambda i, info: (0,) * 6)] + [w_spec] * 4,
            out_specs=[pl.BlockSpec((n_rows // 64, half), lambda i, info: (0, 0)),
                       pl.BlockSpec((3, 16, 128, 128), lambda i, info: (0, 0, 0, 0))],
            scratch_shapes=[pltpu.VMEM((n_rows, half), jnp.bfloat16)] * 2,
        ),
        out_shape=[jax.ShapeDtypeStruct((n_rows // 64, half), jnp.bfloat16),
                   jax.ShapeDtypeStruct((3, 16, 128, 128), jnp.bfloat16)],
        compiler_params=pltpu.CompilerParams(vmem_limit_bytes=48 * 1024 * 1024),
        name="self_attention",
    )(info, gathered, wq, wk, wv, cq)


def kv_kernel(info_ref, m_ref, wk_ref, wv_ref, k_ref, vt_ref):
    @pl.when(pl.program_id(1) < info_ref[3])
    def _():
        rows = m_ref[...]
        k_ref[...] = matmul(rows, wk_ref[...]).astype(jnp.bfloat16)
        vt_ref[...] = jnp.transpose(matmul(rows, wv_ref[...])).astype(jnp.bfloat16)


def memory_kv(info, chip_memory, wk, wv):
    n_rows, width = chip_memory.shape
    half = width // 2
    layers = wk.shape[0]
    w_spec = pl.BlockSpec((None, width, half), lambda l, t, info: (l, 0, info[1]))
    return pl.pallas_call(
        kv_kernel,
        grid_spec=pltpu.PrefetchScalarGridSpec(
            num_scalar_prefetch=1,
            grid=(layers, n_rows // ROW_TILE),
            in_specs=[pl.BlockSpec((ROW_TILE, width), lambda l, t, info: (t, 0)), w_spec, w_spec],
            out_specs=[pl.BlockSpec((None, ROW_TILE, half), lambda l, t, info: (l, t, 0)),
                       pl.BlockSpec((None, half, ROW_TILE), lambda l, t, info: (l, 0, t))],
        ),
        out_shape=[jax.ShapeDtypeStruct((layers, n_rows, half), jnp.bfloat16),
                   jax.ShapeDtypeStruct((layers, half, n_rows), jnp.bfloat16)],
        compiler_params=pltpu.CompilerParams(vmem_limit_bytes=48 * 1024 * 1024),
        name="memory_kv",
    )(info, chip_memory, wk, wv)


def cross_kernel(info_ref, qt_ref, k_ref, vt_ref, out_ref, acc_ref):
    n_valid = info_ref[2]
    n_tiles = info_ref[3]
    n_q = 512
    qt = jnp.concatenate([qt_ref[i] for i in range(4)], axis=1)
    low = lax.broadcasted_iota(jnp.int32, (128, n_q), 0) < HEAD
    zero = jnp.zeros_like(qt)
    ones = jnp.where(lax.broadcasted_iota(jnp.int32, (128, n_q), 0) == 0, 1.0, 0.0).astype(jnp.bfloat16)
    q_heads = (jnp.concatenate([jnp.where(low, qt, zero), ones], axis=0),
               jnp.concatenate([jnp.where(low, zero, qt), ones], axis=0))
    acc_ref[...] = jnp.zeros_like(acc_ref)

    def row_tile(t, carry):
        at = pl.ds(pl.multiple_of(t * ROW_TILE, ROW_TILE), ROW_TILE)
        row = t * ROW_TILE + lax.broadcasted_iota(jnp.int32, (ROW_TILE, 128), 0)
        bias = jnp.where(row < n_valid, 0.0, NEG_BIG).astype(jnp.bfloat16)
        keys = jnp.concatenate([k_ref[at, :], bias], axis=1)
        new = []
        for head in range(2):
            top, total = carry[2 * head], carry[2 * head + 1]
            s = matmul(keys, q_heads[head])
            new_top = jnp.maximum(top, jnp.max(s, axis=0, keepdims=True) * EXP_SCALE)
            w = jnp.exp2(s * EXP_SCALE - new_top)
            fix = jnp.exp2(top - new_top)
            new += [new_top, total * fix + jnp.sum(w, axis=0, keepdims=True)]
            vals = slice(head * HEAD, head * HEAD + HEAD)
            acc_ref[vals, :] = acc_ref[vals, :] * fix + matmul(vt_ref[vals, at], w.astype(jnp.bfloat16))
        return tuple(new)

    init = (jnp.full((1, n_q), NEG_BIG, jnp.float32), jnp.zeros((1, n_q), jnp.float32)) * 2
    t0, l0, t1, l1 = lax.fori_loop(0, n_tiles, row_tile, init)
    out_ref[0:128, :] = acc_ref[...]
    out_ref[128:136, :] = jnp.concatenate([t0, t1, l0, l1, t0, t1, l0, l1], axis=0)


def cross_attention(info, layer, qt, keys, values):
    n_rows = keys.shape[1]
    return pl.pallas_call(
        cross_kernel,
        grid_spec=pltpu.PrefetchScalarGridSpec(
            num_scalar_prefetch=1,
            grid=(3, 4),
            in_specs=[pl.BlockSpec((None, 4, 128, 128), lambda p, j, info: (p, j, 0, 0)),
                      pl.BlockSpec((None, n_rows, 128), lambda p, j, info: (layer, 0, p)),
                      pl.BlockSpec((None, 128, n_rows), lambda p, j, info: (layer, p, 0))],
            out_specs=pl.BlockSpec((None, None, 136, 512), lambda p, j, info: (p, j, 0, 0)),
            scratch_shapes=[pltpu.VMEM((128, 512), jnp.float32)],
        ),
        out_shape=jax.ShapeDtypeStruct((3, 4, 136, 512), jnp.float32),
        compiler_params=pltpu.CompilerParams(vmem_limit_bytes=48 * 1024 * 1024),
        name="cross_attention",
    )(info, qt, keys, values)


def merge(pieces):
    tops = [p[128:130] for p in pieces]
    sums = [p[130:132] for p in pieces]
    top = functools.reduce(jnp.maximum, tops)
    fixes = [jnp.exp2(t - top) for t in tops]
    total = functools.reduce(jnp.add, [f * s for f, s in zip(fixes, sums)])
    outs = []
    for head in range(2):
        rows = slice(head * HEAD, head * HEAD + HEAD)
        outs.append(functools.reduce(jnp.add, [p[rows] * f[head:head + 1] for p, f in zip(pieces, fixes)]))
    return outs, top, total


def merge_kernel(part_ref, att_ref, out_ref, recv1, acc1, recv2, acc2, recv3, turned, mine,
                 send_sem, recv_sem, sib_send, sib_recv):
    pos, core = coords()
    entry_barrier(pos, core)

    def copy(part, phase, dist):
        axis = ORDERS[part][phase]
        peer = shifted(pos, axis, dist)
        src, dst = ((part_ref.at[part, peer[axis]], recv1.at[part, dist - 1]),
                    (acc1.at[part, peer[axis]], recv2.at[part, dist - 1]),
                    (acc2.at[part], recv3.at[part, dist - 1]))[phase]
        return pltpu.make_async_remote_copy(
            src_ref=src, dst_ref=dst, send_sem=send_sem.at[part, phase, dist - 1],
            recv_sem=recv_sem.at[part, phase, dist - 1], device_id=device_of(peer, core), device_id_type=MESH)

    copies = {}

    def start(part, phase):
        for dist in (2, 1, 3):
            copies[part, phase, dist] = copy(part, phase, dist)
            copies[part, phase, dist].start()

    for part in range(3):
        start(part, 0)
    for part in range(3):
        for dist in (1, 2, 3):
            copies[part, 0, dist].wait_recv()
        own = pos[ORDERS[part][0]]
        for b in range(4):
            lanes = slice(b * 128, b * 128 + 128)
            outs, top, total = merge([part_ref[part, own, :, lanes]] + [recv1[part, d, :, lanes] for d in range(3)])
            acc1[part, b, 0:64] = outs[0]
            acc1[part, b, 64:128] = outs[1]
            acc1[part, b, 128:136] = jnp.concatenate([top, total, top, total], axis=0)
        start(part, 1)
    for part in range(3):
        for dist in (1, 2, 3):
            copies[part, 1, dist].wait_recv()
        own = pos[ORDERS[part][1]]
        outs, top, total = merge([acc1[part, own]] + [recv2[part, d] for d in range(3)])
        acc2[part, 0:64] = outs[0]
        acc2[part, 64:128] = outs[1]
        acc2[part, 128:136] = jnp.concatenate([top, total, top, total], axis=0)
        start(part, 2)
    mine[0] = att_ref[...]
    for part in range(3):
        for dist in (1, 2, 3):
            copies[part, 2, dist].wait_recv()
        outs, top, total = merge([acc2[part]] + [recv3[part, d] for d in range(3)])
        turned[part] = jnp.transpose(jnp.concatenate([outs[h] / total[h:h + 1] for h in range(2)], axis=0))
        rows = pl.ds(pl.multiple_of(pos[ORDERS[part][2]] * 32, 32), 32)
        mine[1, :, part * 128:part * 128 + 128] = turned[part, rows, :].astype(jnp.bfloat16)
    n_own = out_ref.shape[2]
    theirs = pl.ds(pl.multiple_of((1 - core) * n_own, n_own), n_own)
    last = pltpu.make_async_remote_copy(
        src_ref=mine.at[:, theirs], dst_ref=out_ref.at[core], send_sem=sib_send, recv_sem=sib_recv,
        device_id=device_of(pos, 1 - core), device_id_type=MESH)
    last.start()
    own_rows = pl.ds(pl.multiple_of(core * n_own, n_own), n_own)
    out_ref[core] = mine[:, own_rows]
    last.wait()
    for one in copies.values():
        one.wait_send()


def merge_parts(partial, att):
    f32, bf16 = jnp.float32, jnp.bfloat16
    n_rows, half = att.shape
    return pl.pallas_call(
        merge_kernel,
        out_shape=jax.ShapeDtypeStruct((2, 2, n_rows // 2, half), bf16),
        in_specs=[VMEM_SPEC] * 2,
        out_specs=VMEM_SPEC,
        scratch_shapes=[pltpu.VMEM((3, 3, 136, 512), f32), pltpu.VMEM((3, 4, 136, 128), f32),
                        pltpu.VMEM((3, 3, 136, 128), f32), pltpu.VMEM((3, 136, 128), f32),
                        pltpu.VMEM((3, 3, 136, 128), f32), pltpu.VMEM((3, 128, 128), f32),
                        pltpu.VMEM((2, n_rows, half), bf16),
                        pltpu.SemaphoreType.DMA((3, 3, 3)), pltpu.SemaphoreType.DMA((3, 3, 3)),
                        pltpu.SemaphoreType.DMA, pltpu.SemaphoreType.DMA],
        compiler_params=pltpu.CompilerParams(collective_id=2, has_side_effects=True),
        name="merge_parts",
    )(partial, att)


def solution(mesh):
    row_spec = P(("dp", "sp"), None)
    full_spec = P()

    def device_step(y_dec, memory, mem_len, norm_gain, self_wq, self_wk, self_wv, self_wo, cross_wq, cross_wk, cross_wv, cross_wo, mlp_gate, mlp_up, mlp_down):
        tq_dev, width = y_dec.shape
        tm_dev = memory.shape[0]
        sp = lax.axis_index("sp")
        chip = sp // 2
        n_valid = jnp.clip(mem_len[0] - chip * (2 * tm_dev), 0, 2 * tm_dev)
        info = jnp.stack([chip, sp % 2, n_valid, (n_valid + ROW_TILE - 1) // ROW_TILE]).astype(jnp.int32)
        chip_memory = swap_memory(memory).reshape(2 * tm_dev, width)
        keys, values = memory_kv(info, chip_memory, cross_wk, cross_wv)
        hidden = y_dec
        for layer in range(norm_gain.shape[0]):
            normed = rms_norm(hidden, norm_gain[layer])
            gathered = gather_rows(normed)
            att, qt = self_attention(info, gathered, layer, self_wq, self_wk, self_wv, cross_wq)
            partial = cross_attention(info, layer, qt, keys, values)
            merged = merge_parts(partial, att)
            merged = merged.transpose(1, 2, 0, 3).reshape(2, tq_dev, width)
            self_part = matmul(merged[0], self_wo[layer])
            cross_part = matmul(merged[1], cross_wo[layer])
            activated = (jax.nn.silu(matmul(normed, mlp_gate[layer])) * matmul(normed, mlp_up[layer])).astype(jnp.bfloat16)
            mlp_part = matmul(activated, mlp_down[layer])
            hidden = (hidden.astype(jnp.float32) + self_part + cross_part + mlp_part).astype(jnp.bfloat16)
        return hidden

    return jax.shard_map(device_step, mesh=mesh, in_specs=(row_spec, row_spec, P("dp")) + (full_spec,) * 12, out_specs=row_spec, check_vma=False)
```

time: 2430 us -> 329 us (0.14)
  waiting for transfers between devices: 2040 us -> 0 us
  Pallas kernels: 0 us -> 301 us
  matrix products: 207 us -> 17.2 us
  local copies, waits for them, and re-layouts: 92.3 us -> 7.92 us
  other arithmetic: 68.8 us -> 0.39 us
    unnamed x16 -> x0, waiting for transfers between devices: 1600 us -> none
    pallas_call x0 -> x10, Pallas kernels: none -> 301 us  [the longest x2 125 us: cross_attention(): pl.pallas_call(cross_kernel, grid_spec=pltpu.PrefetchScalarGridSpec(num_s...]
    all_gather x6 -> x0, waiting for transfers between devices: 231 us -> none  [the longest x2 128 us: device_step(): lax.all_gather(query_local, 'sp', axis=0, tiled=True)]
    pmax x2 -> x0, waiting for transfers between devices: 209 us -> none  [device_step(): top_max = lax.pmax(part_max, 'sp')]
    dot_general x6 -> x0, matrix products: 154 us -> none  [the longest x2 75.2 us: device_step(): jnp.einsum('qkgd,mkd->kgqm', query_cross, key_mem, preferred_element_type...]
    reduce_sum x2 -> x0, other arithmetic: 62.5 us -> none  [device_step(): part_sum = jnp.sum(weights, axis=-1)]
    mul x2 -> x0, local copies, waits for them, and re-layouts: 59.6 us -> none  [device_step(): part_out * rescale[..., None]]
    dot_general x20 -> x8, matrix products: 48 us -> 17.2 us  [matmul(): return jnp.dot(left_mat, right_mat, preferred_element_type=jnp.float32)]
  transfers between devices with their start and end apart: 12 -> 0, of which waited for: 10 -> 0; matrix products, arithmetic and copies ran while one was open for 11% -> 0% of each run, Pallas kernels for 0% -> 0%
where the time goes in v1:
time: 329 us; the launch traced here: 327 us
  Pallas kernels  301 us (91%)
  matrix products  17.2 us (5%)
  local copies, waits for them, and re-layouts  7.92 us (2%)
    pallas_call x2, Pallas kernels, cross_attention(): pl.pallas_call(cross_kernel, grid_spec=pltpu.PrefetchScalarGridSpec(num_s...  125 us
    pallas_call x2, Pallas kernels, merge_parts(): pl.pallas_call(merge_kernel, out_shape=jax.ShapeDtypeStruct((2, 2, n_rows...  62.9 us
    pallas_call x2, Pallas kernels, self_attention(): pl.pallas_call(self_kernel, grid_spec=pltpu.PrefetchScalarGridSpec(num_sc...  49.5 us
    pallas_call x2, Pallas kernels, gather_rows(): pl.pallas_call(gather_kernel, out_shape=jax.ShapeDtypeStruct((3, 4, 4, 4,...  45.2 us
    dot_general x8, matrix products, matmul(): return jnp.dot(left_mat, right_mat, preferred_element_type=jnp.float32)  17.2 us
    pallas_call x1, Pallas kernels, memory_kv(): pl.pallas_call(kv_kernel, grid_spec=pltpu.PrefetchScalarGridSpec(num_scal...  12.5 us

profile of v1, /device:TPU:1, one launch (start us, length us, event | category | flops | bytes accessed | tf_op | source)
XLA Modules:
  0.0 327.3 jit_solution(129321889429824314)
XLA Ops:
  0.8 0.1 pad_add_fusion.info_ref
  0.9 5.8 %swap_memory.1 = bf16[2,1024,768]{2,1,0:T(8,128)(2,1)} custom-call(bf16[1024,768]{1,0:T(8,128)(2,1)} %mem_ref.1), custom_call_target="tpu_custom_call" | custom-call | tf_op jit(solution)/shard_map/swap_memory/pallas_call | solution.py:71
  6.8 1.7 copy-done.4
  8.4 12.5 %memory_kv.1 = (bf16[2,2048,384]{2,1,0:T(8,128)(2,1)}, bf16[2,384,2048]{2,1,0:T(8,128)(2,1)}) custom-call(s32[4]{0:T(128)S(1)} %pad_add_fusion.info_ref, bf16[2048,768]{1,0:T(8,128)(2,1)} %bitcast.109, bf16[2,768,768]{2,1,0:T(8,128)(2,1)S(1)} %copy-done.3, bf16[2,768,768]{2,1,0:T(8,128)(2,1)S(1)} %copy-done.4), custom_call_target="tpu_custom_call" | custom-call | tf_op jit(solution)/shard_map/memory_kv/pallas_call | solution.py:256
  20.9 0.1 fusion.85
  21.1 0.1 fusion.87
  21.1 0.6 copy.31
  21.8 24.1 %gather_rows.2 = bf16[3,4,4,4,2,16,256]{6,5,4,3,2,1,0:T(8,128)(2,1)} custom-call(bf16[3,16,256]{2,1,0:T(8,128)(2,1)} %bitcast.114), custom_call_target="tpu_custom_call" | custom-call | tf_op jit(solution)/shard_map/gather_rows/pallas_call | solution.py:147
  45.8 0.0 copy-start.1
  45.9 1.7 copy-done.1
  47.5 24.9 %self_attention.2 = (bf16[32,384]{1,0:T(8,128)(2,1)S(1)}, bf16[3,16,128,128]{3,2,1,0:T(8,128)(2,1)S(1)}) custom-call(s32[4]{0:T(128)S(1)} %pad_add_fusion.info_ref, bf16[3,4,4,4,32,256]{5,4,3,2,1,0:T(8,128)(2,1)} %bitcast.107, bf16[2,768,768]{2,1,0:T(8,128)(2,1)S(1)} %copy-done.1, bf16[2,768,768]{2,1,0:T(8,128)(2,1)} %wk_ref.5, bf16[2,768,768]{2,1,0:T(8,128)(2,1)} %wv_ref.5, ...), custom_call_target="tpu_custom_call" | custom-call | tf_op jit(solution)/shard_map/self_attention/pallas_call | solution.py:226
  72.4 0.0 copy-start.6
  72.5 62.4 %cross_attention.2.part_ref = f32[3,4,136,512]{3,2,1,0:T(8,128)} custom-call(s32[4]{0:T(128)S(1)} %pad_add_fusion.info_ref, bf16[3,16,128,128]{3,2,1,0:T(8,128)(2,1)S(1)} %get-tuple-element.11.qt_ref, bf16[2,2048,384]{2,1,0:T(8,128)(2,1)S(1)} %copy-done, bf16[2,384,2048]{2,1,0:T(8,128)(2,1)} %get-tuple-element.13.vt_ref), custom_call_target="tpu_custom_call" | custom-call | tf_op jit(solution)/shard_map/cross_attention/pallas_call | solution.py:309
  134.8 31.5 %merge_parts.2 = bf16[2,2,16,384]{3,2,1,0:T(8,128)(2,1)} custom-call(f32[3,4,136,512]{3,2,1,0:T(8,128)} %cross_attention.2.part_ref, bf16[32,384]{1,0:T(8,128)(2,1)} %copy-done.6), custom_call_target="tpu_custom_call" | custom-call | tf_op jit(solution)/shard_map/merge_parts/pallas_call | solution.py:407
  166.4 0.8 fusion.91
  167.2 1.5 fusion.34
  168.8 2.4 fusion.10
  171.2 3.9 %fusion.6 = f32[16,768]{1,0:T(8,128)S(1)} fusion(bf16[2,2048,768]{2,1,0:T(8,128)(2,1)} %param.29, bf16[16,768]{1,0:T(8,128)(2,1)S(1)} %fusion.87, bf16[2,768,2048]{2,1,0:T(8,128)(2,1)} %param.28, f32[16,2048]{1,0:T(8,128)S(1)} %fusion.10), kind=kOutput, calls=%fused_computation.6 | convolution fusion | flops 100859904 | bytes 6496256 | tf_op jit(solution)/shard_map/dot_general | solution.py:22
  175.1 1.7 multiply_reduce_fusion
  176.8 0.1 multiply_convert_fusion
  176.8 0.6 copy.30
  177.5 21.2 %gather_rows.3 = bf16[3,4,4,4,2,16,256]{6,5,4,3,2,1,0:T(8,128)(2,1)} custom-call(bf16[3,16,256]{2,1,0:T(8,128)(2,1)} %bitcast.115), custom_call_target="tpu_custom_call" | custom-call | tf_op jit(solution)/shard_map/gather_rows/pallas_call | solution.py:147
  198.7 0.0 copy-start.2
  198.7 1.7 copy-done.2
  200.3 24.6 %self_attention.3 = (bf16[32,384]{1,0:T(8,128)(2,1)S(1)}, bf16[3,16,128,128]{3,2,1,0:T(8,128)(2,1)S(1)}) custom-call(s32[4]{0:T(128)S(1)} %pad_add_fusion.info_ref, bf16[3,4,4,4,32,256]{5,4,3,2,1,0:T(8,128)(2,1)} %bitcast.108, bf16[2,768,768]{2,1,0:T(8,128)(2,1)S(1)} %copy-done.2, bf16[2,768,768]{2,1,0:T(8,128)(2,1)} %wk_ref.5, bf16[2,768,768]{2,1,0:T(8,128)(2,1)} %wv_ref.5, ...), custom_call_target="tpu_custom_call" | custom-call | tf_op jit(solution)/shard_map/self_attention/pallas_call | solution.py:226
  225.0 62.4 %cross_attention.3.part_ref = f32[3,4,136,512]{3,2,1,0:T(8,128)} custom-call(s32[4]{0:T(128)S(1)} %pad_add_fusion.info_ref, bf16[3,16,128,128]{3,2,1,0:T(8,128)(2,1)S(1)} %get-tuple-element.15.qt_ref, bf16[2,2048,384]{2,1,0:T(8,128)(2,1)S(1)} %copy-done, bf16[2,384,2048]{2,1,0:T(8,128)(2,1)} %get-tuple-element.13.vt_ref), custom_call_target="tpu_custom_call" | custom-call | tf_op jit(solution)/shard_map/cross_attention/pallas_call | solution.py:309
  287.4 31.4 %merge_parts.3 = bf16[2,2,16,384]{3,2,1,0:T(8,128)(2,1)} custom-call(f32[3,4,136,512]{3,2,1,0:T(8,128)} %cross_attention.3.part_ref, bf16[32,384]{1,0:T(8,128)(2,1)} %copy-done.5), custom_call_target="tpu_custom_call" | custom-call | tf_op jit(solution)/shard_map/merge_parts/pallas_call | solution.py:407
  318.8 0.8 fusion.90
  319.6 0.3 fusion.30
  319.9 2.4 fusion.4
  322.3 4.0 %fusion = f32[16,768]{1,0:T(8,128)S(1)} fusion(bf16[2,2048,768]{2,1,0:T(8,128)(2,1)} %param.29, bf16[16,768]{1,0:T(8,128)(2,1)S(1)} %multiply_convert_fusion, bf16[2,768,2048]{2,1,0:T(8,128)(2,1)} %param.28, f32[16,2048]{1,0:T(8,128)S(1)} %fusion.4), kind=kOutput, calls=%fused_computation | convolution fusion | flops 100859904 | bytes 6496256 | tf_op jit(solution)/shard_map/dot_general | solution.py:22
  326.4 0.9 fusion.60
  (27 shorter events, 0.2 us)
Async XLA Ops:
  0.0 6.8 %copy-start.3 = (bf16[2,768,768]{2,1,0:T(8,128)(2,1)S(1)}, bf16[2,768,768]{2,1,0:T(8,128)(2,1)}, u32[]{:S(2)}) copy-start(bf16[2,768,768]{2,1,0:T(8,128)(2,1)} %wk_ref.4) | copy-start | bytes 7077892
  6.8 1.7 copy-start.4
  8.4 12.5 %copy-start.10 = (bf16[2,768]{1,0:T(2,128)(2,1)S(1)}, bf16[2,768]{1,0:T(2,128)(2,1)}, u32[]{:S(2)}) copy-start(bf16[2,768]{1,0:T(2,128)(2,1)} %param.18) | copy-start | bytes 9220
  8.4 12.5 %copy-start.9 = (bf16[16,768]{1,0:T(8,128)(2,1)S(1)}, bf16[16,768]{1,0:T(8,128)(2,1)}, u32[]{:S(2)}) copy-start(bf16[16,768]{1,0:T(8,128)(2,1)} %param.15) | copy-start | bytes 73732
  45.8 1.7 copy-start.1
  47.5 24.9 %copy-start = (bf16[2,2048,384]{2,1,0:T(8,128)(2,1)S(1)}, bf16[2,2048,384]{2,1,0:T(8,128)(2,1)}, u32[]{:S(2)}) copy-start(bf16[2,2048,384]{2,1,0:T(8,128)(2,1)} %get-tuple-element.12.k_ref) | copy-start | bytes 9437188
  72.4 62.4 %copy-start.6 = (bf16[32,384]{1,0:T(8,128)(2,1)}, bf16[32,384]{1,0:T(8,128)(2,1)S(1)}, u32[]{:S(2)}) copy-start(bf16[32,384]{1,0:T(8,128)(2,1)S(1)} %get-tuple-element.14.att_ref) | copy-start | bytes 73732
  198.7 1.7 copy-start.2
  225.0 62.4 %copy-start.5 = (bf16[32,384]{1,0:T(8,128)(2,1)}, bf16[32,384]{1,0:T(8,128)(2,1)S(1)}, u32[]{:S(2)}) copy-start(bf16[32,384]{1,0:T(8,128)(2,1)S(1)} %get-tuple-element.16.att_ref) | copy-start | bytes 73732
  287.4 32.2 %copy-start.7 = (bf16[2,768,768]{2,1,0:T(8,128)(2,1)S(1)}, bf16[2,768,768]{2,1,0:T(8,128)(2,1)}, u32[]{:S(2)}) copy-start(bf16[2,768,768]{2,1,0:T(8,128)(2,1)} %param.26) | copy-start | bytes 7077892
  322.3 4.0 %copy-start.8 = (bf16[2,768,768]{2,1,0:T(8,128)(2,1)S(1)}, bf16[2,768,768]{2,1,0:T(8,128)(2,1)}, u32[]{:S(2)}) copy-start(bf16[2,768,768]{2,1,0:T(8,128)(2,1)} %param.22) | copy-start | bytes 7077892
